TPU v7x, 32 devices: a whole 2x2x4 slice. The times are simulated.
32 devices in a mesh: vblk: 4 (over y, x), samp: 8 (over z, core).
Axes of the slice: x: 2, y: 2, z: 4, core: 2. Of those that a mesh axis runs over, the one named last changes fastest.
Arguments:
- vectors: bfloat16 [1024, 32768], P('vblk', 'samp'), may hold values from 0 to 2, as said below
- partner: bfloat16 [1024, 32768], P('vblk', 'samp'), may hold values from 0 to 2, as said below
- next_rows: bfloat16 [1024, 32768], P(('vblk', 'samp')), may hold values from 0 to 2, as said below
Outputs:
- metric: float32 [1024, 256], P('vblk', 'samp')
- next_block: bfloat16 [1024, 32768], P('vblk', 'samp')
Inputs may be any that keep to these rules, and one draw needn't show every extreme that they name: vectors: real expected allele dosages, every entry positive. partner: real expected allele dosages, every entry positive. next_rows: real expected allele dosages, every entry positive.
All inputs are finite; a program needn't handle non-finite values.
Results may differ from a plain program's by a relative error of at most 0.0004.
Values may be sent and summed in bfloat16 or wider, within the bound.
A program may use at most 64 MiB of HBM per device.

v0:
```python
import jax
import jax.numpy as jnp
from jax import lax
from jax.sharding import PartitionSpec as P


def from_behind(value, axis, steps):
    count = lax.axis_size(axis)
    pairs = [(source, (source + steps) % count) for source in range(count)]
    return lax.ppermute(value, axis, pairs)


def pair_terms(row_block, col_block):
    row_count = row_block.shape[0]
    grouped = row_block.reshape(row_count // 8, 8, row_block.shape[1])

    def group_sums(row_group):
        return jnp.sum(
            jnp.minimum(row_group[:, None, :], col_block[None, :, :]), axis=2, dtype=jnp.float32
        )

    numerators = lax.map(group_sums, grouped).reshape(row_count, col_block.shape[0])
    row_totals = jnp.sum(row_block, axis=1, dtype=jnp.float32)[:, None]
    col_totals = jnp.sum(col_block, axis=1, dtype=jnp.float32)[None, :]
    return (numerators, row_totals, col_totals)


def body(vectors, partner, next_rows):
    next_block = lax.all_to_all(next_rows, "samp", split_axis=1, concat_axis=0, tiled=True)
    arrived = from_behind(partner, "vblk", 1)
    numerators, row_totals, col_totals = pair_terms(vectors, arrived)
    numerators, col_totals = (
        lax.psum_scatter(numerators, "samp", scatter_dimension=1, tiled=True),
        lax.psum_scatter(col_totals, "samp", scatter_dimension=1, tiled=True),
    )
    row_totals = lax.psum(row_totals, "samp")
    metric = 2.0 * numerators / (row_totals + col_totals)
    return (metric, next_block)


def solution(mesh):
    in_specs = (P("vblk", "samp"), P("vblk", "samp"), P(("vblk", "samp"), None))
    out_specs = (P("vblk", "samp"), P("vblk", "samp"))
    return jax.shard_map(body, mesh=mesh, in_specs=in_specs, out_specs=out_specs, check_vma=False)
```

profile of v0, /device:TPU:0, one launch (start us, length us, event | category | flops | bytes accessed | tf_op | source)
XLA Modules:
  0.0 215.1 jit_solution(9733914594376344194)
XLA Ops:
  7.2 3.0 %collective-permute-start = (bf16[256,4096]{1,0:T(8,128)(2,1)}, bf16[256,4096]{1,0:T(8,128)(2,1)S(1)}, u32[]{:S(2)}, u32[]{:S(2)}) collective-permute-start(bf16[256,4096]{1,0:T(8,128)(2,1)} %param.6), channel_id=1, source_target_pairs={{0,8},{8,16},{16,24},{24,0},{1,9},{9,17},{17,25},{25,1},{2,10},{10... | collective-permute-start | bytes 6291464 | tf_op jit(solution)/shard_map/ppermute | solution.py:10
  10.2 3.1 %copy.19 = bf16[4,8,8,4096]{3,2,0,1:T(8,128)(2,1)} copy(bf16[4,8,8,4096]{3,2,1,0:T(8,128)(2,1)} %bitcast.26) | data formatting | bytes 4194304 | tf_op jit(solution)/shard_map/all_to_all | solution.py:29
  13.3 4.9 %all-to-all-start = ((bf16[32,8,4096]{2,0,1:T(8,128)(2,1)}), bf16[32,8,4096]{2,0,1:T(8,128)(2,1)}, u32[]{:S(2)}, u32[]{:S(2)}) async-start(bf16[32,8,4096]{2,0,1:T(8,128)(2,1)} %bitcast.23), calls=%async_computation | async-start | bytes 4194304 | tf_op jit(solution)/shard_map/all_to_all | solution.py:29
  18.2 38.7 %collective-permute-done = bf16[256,4096]{1,0:T(8,128)(2,1)S(1)} collective-permute-done((bf16[256,4096]{1,0:T(8,128)(2,1)}, bf16[256,4096]{1,0:T(8,128)(2,1)S(1)}, u32[]{:S(2)}, u32[]{:S(2)}) %collective-permute-start) | collective-permute-done | bytes 2097184 | tf_op jit(solution)/shard_map/ppermute | solution.py:10
  58.2 112.9 %while.10 = (s32[]{:T(128)}, f32[32,8,256]{2,1,0:T(8,128)S(1)}, bf16[32,8,4096]{2,1,0:T(8,128)(2,1)}, bf16[256,4096]{1,0:T(8,128)(2,1)S(1)}, s32[]{:T(128)}) while((s32[]{:T(128)}, f32[32,8,256]{2,1,0:T(8,128)S(1)}, bf16[32,8,4096]{2,1,0:T(8,128)(2,1)}, bf16[256,4096]{1,0:T(8,128)(2,1)S(1)}, s32[]{:T(128)}) %tuple.34), condition=%wide.region_2.3_spmd, body=%wide.region_0.2_spmd.sunk | while | flops 25163776 | bytes 2318405 | solution.py:22
  59.1 2.7 %convert_reduce_fusion.4 = f32[8,256]{1,0:T(8,128)S(1)} fusion(bf16[256,4096]{1,0:T(8,128)(2,1)S(1)} %get-tuple-element.77, bf16[8,4096]{1,0:T(8,128)(2,1)S(1)} %dynamic-slice_bitcast_fusion.2), kind=kLoop, calls=%fused_computation.clone.1 | loop fusion | flops 25163776 | bytes 2170880 | tf_op jit(solution)/shard_map/while/body/eval_jaxpr/reduce_sum | solution.py:18
  62.6 2.7 %convert_reduce_fusion.4 = f32[8,256]{1,0:T(8,128)S(1)} fusion(bf16[256,4096]{1,0:T(8,128)(2,1)S(1)} %get-tuple-element.77, bf16[8,4096]{1,0:T(8,128)(2,1)S(1)} %dynamic-slice_bitcast_fusion.2), kind=kLoop, calls=%fused_computation.clone.1 | loop fusion | flops 25163776 | bytes 2170880 | tf_op jit(solution)/shard_map/while/body/eval_jaxpr/reduce_sum | solution.py:18
  66.1 2.7 %convert_reduce_fusion.4 = f32[8,256]{1,0:T(8,128)S(1)} fusion(bf16[256,4096]{1,0:T(8,128)(2,1)S(1)} %get-tuple-element.77, bf16[8,4096]{1,0:T(8,128)(2,1)S(1)} %dynamic-slice_bitcast_fusion.2), kind=kLoop, calls=%fused_computation.clone.1 | loop fusion | flops 25163776 | bytes 2170880 | tf_op jit(solution)/shard_map/while/body/eval_jaxpr/reduce_sum | solution.py:18
  69.7 2.7 %convert_reduce_fusion.4 = f32[8,256]{1,0:T(8,128)S(1)} fusion(bf16[256,4096]{1,0:T(8,128)(2,1)S(1)} %get-tuple-element.77, bf16[8,4096]{1,0:T(8,128)(2,1)S(1)} %dynamic-slice_bitcast_fusion.2), kind=kLoop, calls=%fused_computation.clone.1 | loop fusion | flops 25163776 | bytes 2170880 | tf_op jit(solution)/shard_map/while/body/eval_jaxpr/reduce_sum | solution.py:18
  73.2 2.7 %convert_reduce_fusion.4 = f32[8,256]{1,0:T(8,128)S(1)} fusion(bf16[256,4096]{1,0:T(8,128)(2,1)S(1)} %get-tuple-element.77, bf16[8,4096]{1,0:T(8,128)(2,1)S(1)} %dynamic-slice_bitcast_fusion.2), kind=kLoop, calls=%fused_computation.clone.1 | loop fusion | flops 25163776 | bytes 2170880 | tf_op jit(solution)/shard_map/while/body/eval_jaxpr/reduce_sum | solution.py:18
  76.7 2.7 %convert_reduce_fusion.4 = f32[8,256]{1,0:T(8,128)S(1)} fusion(bf16[256,4096]{1,0:T(8,128)(2,1)S(1)} %get-tuple-element.77, bf16[8,4096]{1,0:T(8,128)(2,1)S(1)} %dynamic-slice_bitcast_fusion.2), kind=kLoop, calls=%fused_computation.clone.1 | loop fusion | flops 25163776 | bytes 2170880 | tf_op jit(solution)/shard_map/while/body/eval_jaxpr/reduce_sum | solution.py:18
  80.2 2.7 %convert_reduce_fusion.4 = f32[8,256]{1,0:T(8,128)S(1)} fusion(bf16[256,4096]{1,0:T(8,128)(2,1)S(1)} %get-tuple-element.77, bf16[8,4096]{1,0:T(8,128)(2,1)S(1)} %dynamic-slice_bitcast_fusion.2), kind=kLoop, calls=%fused_computation.clone.1 | loop fusion | flops 25163776 | bytes 2170880 | tf_op jit(solution)/shard_map/while/body/eval_jaxpr/reduce_sum | solution.py:18
  83.8 2.7 %convert_reduce_fusion.4 = f32[8,256]{1,0:T(8,128)S(1)} fusion(bf16[256,4096]{1,0:T(8,128)(2,1)S(1)} %get-tuple-element.77, bf16[8,4096]{1,0:T(8,128)(2,1)S(1)} %dynamic-slice_bitcast_fusion.2), kind=kLoop, calls=%fused_computation.clone.1 | loop fusion | flops 25163776 | bytes 2170880 | tf_op jit(solution)/shard_map/while/body/eval_jaxpr/reduce_sum | solution.py:18
  87.3 2.7 %convert_reduce_fusion.4 = f32[8,256]{1,0:T(8,128)S(1)} fusion(bf16[256,4096]{1,0:T(8,128)(2,1)S(1)} %get-tuple-element.77, bf16[8,4096]{1,0:T(8,128)(2,1)S(1)} %dynamic-slice_bitcast_fusion.2), kind=kLoop, calls=%fused_computation.clone.1 | loop fusion | flops 25163776 | bytes 2170880 | tf_op jit(solution)/shard_map/while/body/eval_jaxpr/reduce_sum | solution.py:18
  90.8 2.7 %convert_reduce_fusion.4 = f32[8,256]{1,0:T(8,128)S(1)} fusion(bf16[256,4096]{1,0:T(8,128)(2,1)S(1)} %get-tuple-element.77, bf16[8,4096]{1,0:T(8,128)(2,1)S(1)} %dynamic-slice_bitcast_fusion.2), kind=kLoop, calls=%fused_computation.clone.1 | loop fusion | flops 25163776 | bytes 2170880 | tf_op jit(solution)/shard_map/while/body/eval_jaxpr/reduce_sum | solution.py:18
  94.4 2.7 %convert_reduce_fusion.4 = f32[8,256]{1,0:T(8,128)S(1)} fusion(bf16[256,4096]{1,0:T(8,128)(2,1)S(1)} %get-tuple-element.77, bf16[8,4096]{1,0:T(8,128)(2,1)S(1)} %dynamic-slice_bitcast_fusion.2), kind=kLoop, calls=%fused_computation.clone.1 | loop fusion | flops 25163776 | bytes 2170880 | tf_op jit(solution)/shard_map/while/body/eval_jaxpr/reduce_sum | solution.py:18
  97.9 2.7 %convert_reduce_fusion.4 = f32[8,256]{1,0:T(8,128)S(1)} fusion(bf16[256,4096]{1,0:T(8,128)(2,1)S(1)} %get-tuple-element.77, bf16[8,4096]{1,0:T(8,128)(2,1)S(1)} %dynamic-slice_bitcast_fusion.2), kind=kLoop, calls=%fused_computation.clone.1 | loop fusion | flops 25163776 | bytes 2170880 | tf_op jit(solution)/shard_map/while/body/eval_jaxpr/reduce_sum | solution.py:18
  101.4 2.7 %convert_reduce_fusion.4 = f32[8,256]{1,0:T(8,128)S(1)} fusion(bf16[256,4096]{1,0:T(8,128)(2,1)S(1)} %get-tuple-element.77, bf16[8,4096]{1,0:T(8,128)(2,1)S(1)} %dynamic-slice_bitcast_fusion.2), kind=kLoop, calls=%fused_computation.clone.1 | loop fusion | flops 25163776 | bytes 2170880 | tf_op jit(solution)/shard_map/while/body/eval_jaxpr/reduce_sum | solution.py:18
  105.0 2.7 %convert_reduce_fusion.4 = f32[8,256]{1,0:T(8,128)S(1)} fusion(bf16[256,4096]{1,0:T(8,128)(2,1)S(1)} %get-tuple-element.77, bf16[8,4096]{1,0:T(8,128)(2,1)S(1)} %dynamic-slice_bitcast_fusion.2), kind=kLoop, calls=%fused_computation.clone.1 | loop fusion | flops 25163776 | bytes 2170880 | tf_op jit(solution)/shard_map/while/body/eval_jaxpr/reduce_sum | solution.py:18
  108.5 2.7 %convert_reduce_fusion.4 = f32[8,256]{1,0:T(8,128)S(1)} fusion(bf16[256,4096]{1,0:T(8,128)(2,1)S(1)} %get-tuple-element.77, bf16[8,4096]{1,0:T(8,128)(2,1)S(1)} %dynamic-slice_bitcast_fusion.2), kind=kLoop, calls=%fused_computation.clone.1 | loop fusion | flops 25163776 | bytes 2170880 | tf_op jit(solution)/shard_map/while/body/eval_jaxpr/reduce_sum | solution.py:18
  112.0 2.7 %convert_reduce_fusion.4 = f32[8,256]{1,0:T(8,128)S(1)} fusion(bf16[256,4096]{1,0:T(8,128)(2,1)S(1)} %get-tuple-element.77, bf16[8,4096]{1,0:T(8,128)(2,1)S(1)} %dynamic-slice_bitcast_fusion.2), kind=kLoop, calls=%fused_computation.clone.1 | loop fusion | flops 25163776 | bytes 2170880 | tf_op jit(solution)/shard_map/while/body/eval_jaxpr/reduce_sum | solution.py:18
  115.5 2.7 %convert_reduce_fusion.4 = f32[8,256]{1,0:T(8,128)S(1)} fusion(bf16[256,4096]{1,0:T(8,128)(2,1)S(1)} %get-tuple-element.77, bf16[8,4096]{1,0:T(8,128)(2,1)S(1)} %dynamic-slice_bitcast_fusion.2), kind=kLoop, calls=%fused_computation.clone.1 | loop fusion | flops 25163776 | bytes 2170880 | tf_op jit(solution)/shard_map/while/body/eval_jaxpr/reduce_sum | solution.py:18
  119.1 2.7 %convert_reduce_fusion.4 = f32[8,256]{1,0:T(8,128)S(1)} fusion(bf16[256,4096]{1,0:T(8,128)(2,1)S(1)} %get-tuple-element.77, bf16[8,4096]{1,0:T(8,128)(2,1)S(1)} %dynamic-slice_bitcast_fusion.2), kind=kLoop, calls=%fused_computation.clone.1 | loop fusion | flops 25163776 | bytes 2170880 | tf_op jit(solution)/shard_map/while/body/eval_jaxpr/reduce_sum | solution.py:18
  122.6 2.7 %convert_reduce_fusion.4 = f32[8,256]{1,0:T(8,128)S(1)} fusion(bf16[256,4096]{1,0:T(8,128)(2,1)S(1)} %get-tuple-element.77, bf16[8,4096]{1,0:T(8,128)(2,1)S(1)} %dynamic-slice_bitcast_fusion.2), kind=kLoop, calls=%fused_computation.clone.1 | loop fusion | flops 25163776 | bytes 2170880 | tf_op jit(solution)/shard_map/while/body/eval_jaxpr/reduce_sum | solution.py:18
  126.1 2.7 %convert_reduce_fusion.4 = f32[8,256]{1,0:T(8,128)S(1)} fusion(bf16[256,4096]{1,0:T(8,128)(2,1)S(1)} %get-tuple-element.77, bf16[8,4096]{1,0:T(8,128)(2,1)S(1)} %dynamic-slice_bitcast_fusion.2), kind=kLoop, calls=%fused_computation.clone.1 | loop fusion | flops 25163776 | bytes 2170880 | tf_op jit(solution)/shard_map/while/body/eval_jaxpr/reduce_sum | solution.py:18
  129.7 2.7 %convert_reduce_fusion.4 = f32[8,256]{1,0:T(8,128)S(1)} fusion(bf16[256,4096]{1,0:T(8,128)(2,1)S(1)} %get-tuple-element.77, bf16[8,4096]{1,0:T(8,128)(2,1)S(1)} %dynamic-slice_bitcast_fusion.2), kind=kLoop, calls=%fused_computation.clone.1 | loop fusion | flops 25163776 | bytes 2170880 | tf_op jit(solution)/shard_map/while/body/eval_jaxpr/reduce_sum | solution.py:18
  140.2 2.7 %convert_reduce_fusion.4 = f32[8,256]{1,0:T(8,128)S(1)} fusion(bf16[256,4096]{1,0:T(8,128)(2,1)S(1)} %get-tuple-element.77, bf16[8,4096]{1,0:T(8,128)(2,1)S(1)} %dynamic-slice_bitcast_fusion.2), kind=kLoop, calls=%fused_computation.clone.1 | loop fusion | flops 25163776 | bytes 2170880 | tf_op jit(solution)/shard_map/while/body/eval_jaxpr/reduce_sum | solution.py:18
  150.8 2.7 %convert_reduce_fusion.4 = f32[8,256]{1,0:T(8,128)S(1)} fusion(bf16[256,4096]{1,0:T(8,128)(2,1)S(1)} %get-tuple-element.77, bf16[8,4096]{1,0:T(8,128)(2,1)S(1)} %dynamic-slice_bitcast_fusion.2), kind=kLoop, calls=%fused_computation.clone.1 | loop fusion | flops 25163776 | bytes 2170880 | tf_op jit(solution)/shard_map/while/body/eval_jaxpr/reduce_sum | solution.py:18
  161.4 2.7 %convert_reduce_fusion.4 = f32[8,256]{1,0:T(8,128)S(1)} fusion(bf16[256,4096]{1,0:T(8,128)(2,1)S(1)} %get-tuple-element.77, bf16[8,4096]{1,0:T(8,128)(2,1)S(1)} %dynamic-slice_bitcast_fusion.2), kind=kLoop, calls=%fused_computation.clone.1 | loop fusion | flops 25163776 | bytes 2170880 | tf_op jit(solution)/shard_map/while/body/eval_jaxpr/reduce_sum | solution.py:18
  174.0 16.0 %psum.7 = f32[256]{0:T(256)S(1)} all-reduce(f32[256]{0:T(256)S(1)} %convert_reduce_fusion.2), channel_id=1, replica_groups=mesh['vblk'=4,'samp'=8] {'samp'}, use_global_device_ids=true, to_apply=%region_5.6 | all-reduce | flops 256 | bytes 2048 | tf_op jit(solution)/shard_map/psum | solution.py:36
  190.8 12.7 %reduce-scatter.7.cloned.1.call-done = f32[32,256]{1,0:T(8,128)} async-done(((f32[256,256]{1,0:T(8,128)}), f32[32,256]{1,0:T(8,128)}) %reduce-scatter.7.cloned.1.call-update) | async-done | bytes 32784
  205.2 3.1 %copy.30 = bf16[256,4096]{1,0:T(8,128)(2,1)} copy(bf16[256,4096]{1,0:T(8,128)(2,1)} %bitcast.11) | data formatting | bytes 4194304
  (87 shorter events, 55.1 us)
Async XLA Ops:
  7.2 49.8 %collective-permute-start = (bf16[256,4096]{1,0:T(8,128)(2,1)}, bf16[256,4096]{1,0:T(8,128)(2,1)S(1)}, u32[]{:S(2)}, u32[]{:S(2)}) collective-permute-start(bf16[256,4096]{1,0:T(8,128)(2,1)} %param.6), channel_id=1, source_target_pairs={{0,8},{8,16},{16,24},{24,0},{1,9},{9,17},{17,25},{25,1},{2,10},{10... | collective-permute-start | bytes 6291464 | tf_op jit(solution)/shard_map/ppermute | solution.py:10
  13.3 191.9 %all-to-all-start = ((bf16[32,8,4096]{2,0,1:T(8,128)(2,1)}), bf16[32,8,4096]{2,0,1:T(8,128)(2,1)}, u32[]{:S(2)}, u32[]{:S(2)}) async-start(bf16[32,8,4096]{2,0,1:T(8,128)(2,1)} %bitcast.23), calls=%async_computation | async-start | bytes 4194304 | tf_op jit(solution)/shard_map/all_to_all | solution.py:29
  18.2 171.8 %reduce-scatter.9.cloned.1.call-start = ((), (), s32[]{:S(2)}) async-start(), calls=%async_computation.4 | async-start | bytes 147456
  58.2 145.3 %reduce-scatter.7.cloned.1.call-start = ((), (), s32[]{:S(2)}) async-start(), calls=%async_computation.3 | async-start | bytes 294912
Sparse Core Ops, SparseCore 0:
  58.3 31.0 reduce-scatter.8
  172.2 31.2 reduce-scatter.6
where the time goes:
time: 217 us; the launch traced here: 215 us
  other arithmetic  87.2 us (40%)
  waiting for transfers between devices  51.5 us (24%)
  local copies, waits for them, and re-layouts  37.6 us (17%)
  blocking collectives  16 us (7%)
  between operations  14.1 us (6%)
  starting transfers between devices  7.97 us (4%)
    reduce_sum x32, other arithmetic, group_sums(): jnp.sum(jnp.minimum(row_group[:, None, :], col_block[None, :, :]), axis=2...  84.8 us
    ppermute x1, waiting for transfers between devices, from_behind(): return lax.ppermute(value, axis, pairs)  38.7 us
    min x32, local copies, waits for them, and re-layouts, group_sums(): jnp.minimum(row_group[:, None, :], col_block[None, :, :])  27.1 us
    psum x1, blocking collectives, body(): row_totals = lax.psum(row_totals, 'samp')  16 us
    unnamed x4, waiting for transfers between devices  12.8 us
    unnamed x6, local copies, waits for them, and re-layouts  7.12 us
    all_to_all x1, starting transfers between devices, body(): lax.all_to_all(next_rows, 'samp', split_axis=1, concat_axis=0, tiled=True)  4.88 us
  transfers between devices with their start and end apart: 4, of which 2 were waited for; matrix products, arithmetic and copies ran while one was open for 57% of the time, Pallas kernels for 0%

commit v1 on v0

--- a/solution.py
+++ b/solution.py
@@ -1,7 +1,19 @@
+import functools
+
 import jax
 import jax.numpy as jnp
 from jax import lax
+from jax.experimental import pallas as pl
+from jax.experimental.pallas import tpu as pltpu
 from jax.sharding import PartitionSpec as P
+
+MESH = pl.DeviceIdType.MESH
+SUB = 16
+LANES = 128
+TREE = 8
+KTILE = 256
+ROWS_PER_DOT = 256
+VMEM_BYTES = 60 * 1024 * 1024
 
 
 def from_behind(value, axis, steps):
@@ -25,7 +37,7 @@
     return (numerators, row_totals, col_totals)
 
 
-def body(vectors, partner, next_rows):
+def plain_body(vectors, partner, next_rows):
     next_block = lax.all_to_all(next_rows, "samp", split_axis=1, concat_axis=0, tiled=True)
     arrived = from_behind(partner, "vblk", 1)
     numerators, row_totals, col_totals = pair_terms(vectors, arrived)
@@ -38,7 +50,240 @@
     return (metric, next_block)
 
 
+def flipped(index, mask, count):
+    out = 0
+    bit = 1
+    while bit < count:
+        out = out + lax.rem(lax.div(index, bit) + lax.div(mask, bit), 2) * bit
+        bit *= 2
+    return out
+
+
+def tree_sum(values):
+    while len(values) > 1:
+        values = [values[i] + values[i + 1] for i in range(0, len(values), 2)]
+    return values[0]
+
+
+def row_sums(block):
+    ones = jnp.ones((8, block.shape[1]), jnp.bfloat16)
+    return lax.dot_general(
+        ones, block, (((1,), (1,)), ((), ())), preferred_element_type=jnp.float32
+    )
+
+
+def kernel(
+    n_vblk, n_samp,
+    vec_hbm, partner_hbm, next_hbm,
+    total_ref, block_hbm,
+    vec, wide, arrived, own_piece, part, part_in,
+    vec_sem, piece_sem, pair_send, pair_recv, next_send, next_recv, part_send, part_recv,
+):
+    b = lax.axis_index("vblk")
+    s = lax.axis_index("samp")
+    up = lax.rem(b + 1, n_vblk)
+    down = lax.rem(b + n_vblk - 1, n_vblk)
+    row_count, samples = vec.shape
+    cols = row_count // n_samp
+    next_count = next_hbm.shape[0]
+    group = ROWS_PER_DOT // cols
+    span = samples // TREE
+
+    vec_copy = pltpu.make_async_copy(vec_hbm, vec, vec_sem)
+    vec_copy.start()
+    own_in = pltpu.make_async_copy(
+        next_hbm.at[:, pl.ds(pl.multiple_of(s * samples, samples), samples)],
+        own_piece, piece_sem.at[0],
+    )
+    own_in.start()
+
+    barrier = pltpu.get_barrier_semaphore()
+    for neighbour in (up, down):
+        pl.semaphore_signal(barrier, inc=1, device_id=(neighbour, s), device_id_type=MESH)
+    for m in range(1, n_samp):
+        pl.semaphore_signal(
+            barrier, inc=1, device_id=(b, flipped(s, m, n_samp)), device_id_type=MESH
+        )
+    pl.semaphore_wait(barrier, n_samp + 1)
+
+    def pair_copy(i):
+        owner = flipped(s, n_samp - 1 - i, n_samp)
+        return pltpu.make_async_remote_copy(
+            src_ref=partner_hbm.at[pl.ds(pl.multiple_of(owner * cols, cols), cols), :],
+            dst_ref=arrived.at[i],
+            send_sem=pair_send.at[i], recv_sem=pair_recv.at[i],
+            device_id=(up, s), device_id_type=MESH,
+        )
+
+    def next_copy(m):
+        peer = flipped(s, m, n_samp)
+        return pltpu.make_async_remote_copy(
+            src_ref=next_hbm.at[:, pl.ds(pl.multiple_of(peer * samples, samples), samples)],
+            dst_ref=block_hbm.at[pl.ds(pl.multiple_of(s * next_count, next_count), next_count), :],
+            send_sem=next_send.at[m], recv_sem=next_recv.at[m],
+            device_id=(b, peer), device_id_type=MESH,
+        )
+
+    def part_copy(i):
+        peer = flipped(s, n_samp - 1 - i, n_samp)
+        return pltpu.make_async_remote_copy(
+            src_ref=part.at[i], dst_ref=part_in.at[i],
+            send_sem=part_send.at[i], recv_sem=part_recv.at[i],
+            device_id=(b, peer), device_id_type=MESH,
+        )
+
+    for i in range(n_samp):
+        pair_copy(i).start()
+    for m in range(1, n_samp):
+        next_copy(m).start()
+
+    own_in.wait()
+    own_out = pltpu.make_async_copy(
+        own_piece,
+        block_hbm.at[pl.ds(pl.multiple_of(s * next_count, next_count), next_count), :],
+        piece_sem.at[1],
+    )
+    own_out.start()
+
+    vec_copy.wait()
+
+    def widen(t, carry):
+        first = pl.multiple_of(t * SUB, SUB)
+        for c in range(samples // LANES):
+            lanes = pl.ds(c * LANES, LANES)
+            rows = vec[pl.ds(first, SUB), lanes].astype(jnp.float32)
+            for r in range(SUB):
+                wide[first + r, :, lanes] = jnp.broadcast_to(
+                    rows[r:r + 1, :], (SUB, LANES)
+                ).astype(jnp.bfloat16)
+        return carry
+
+    lax.fori_loop(0, row_count // SUB, widen, 0)
+
+    own_totals = row_sums(vec[:, pl.ds(0, KTILE)])
+    own_totals = lax.fori_loop(
+        1, samples // KTILE,
+        lambda k, acc: acc + row_sums(vec[:, pl.ds(pl.multiple_of(k * KTILE, KTILE), KTILE)]),
+        own_totals,
+    )
+
+    groups = row_count // group
+
+    def chunk(i, carry):
+        pair_copy(i).wait_recv()
+
+        def one_group(q):
+            out = None
+            for kt in range(span // KTILE):
+                halves = []
+                for h in range(KTILE // LANES):
+                    at = [g * span + kt * KTILE + h * LANES for g in range(TREE)]
+                    theirs = [
+                        [arrived[i, pl.ds(j * SUB, SUB), pl.ds(o, LANES)] for o in at]
+                        for j in range(cols // SUB)
+                    ]
+                    pieces = []
+                    for r in range(group):
+                        mine = [wide[q * group + r, :, pl.ds(o, LANES)] for o in at]
+                        for j in range(cols // SUB):
+                            pieces.append(
+                                tree_sum([jnp.minimum(x, y) for x, y in zip(mine, theirs[j])])
+                            )
+                    halves.append(jnp.concatenate(pieces, axis=0))
+                sums = row_sums(jnp.concatenate(halves, axis=1))
+                out = sums if out is None else out + sums
+            part[i, pl.ds(q, 1), :] = out[0:1, :]
+
+        def groups_step(q, c):
+            one_group(q)
+            return c
+
+        lax.fori_loop(0, groups, groups_step, 0)
+        part[i, pl.ds(groups, 8), :] = own_totals
+        part[i, pl.ds(groups + 1, 1), pl.ds(0, cols)] = row_sums(arrived[i])[0:1, :]
+
+        @pl.when(i < n_samp - 1)
+        def _():
+            part_copy(i).start()
+
+        return carry
+
+    lax.fori_loop(0, n_samp, chunk, 0)
+
+    total = part[n_samp - 1]
+    for i in range(n_samp - 1):
+        part_copy(i).wait_recv()
+        total = total + part_in[i]
+    total_ref[...] = total
+
+    for i in range(n_samp):
+        pair_copy(i).wait_send()
+    for i in range(n_samp - 1):
+        part_copy(i).wait_send()
+    for m in range(1, n_samp):
+        next_copy(m).wait()
+    own_out.wait()
+
+
+def fused_body(n_vblk, n_samp, vectors, partner, next_rows):
+    rows, samples = vectors.shape
+    cols = rows // n_samp
+    groups = rows * cols // ROWS_PER_DOT
+    part_rows = groups + 8
+    next_count = next_rows.shape[0]
+    hbm = pl.BlockSpec(memory_space=pl.ANY)
+    dma = pltpu.SemaphoreType.DMA
+    total, next_block = pl.pallas_call(
+        functools.partial(kernel, n_vblk, n_samp),
+        out_shape=(
+            jax.ShapeDtypeStruct((part_rows, ROWS_PER_DOT), jnp.float32),
+            jax.ShapeDtypeStruct((next_count * n_samp, samples), next_rows.dtype),
+        ),
+        in_specs=[hbm, hbm, hbm],
+        out_specs=(pl.BlockSpec(memory_space=pltpu.VMEM), hbm),
+        scratch_shapes=[
+            pltpu.VMEM((rows, samples), jnp.bfloat16),
+            pltpu.VMEM((rows, SUB, samples), jnp.bfloat16),
+            pltpu.VMEM((n_samp, cols, samples), jnp.bfloat16),
+            pltpu.VMEM((next_count, samples), jnp.bfloat16),
+            pltpu.VMEM((n_samp, part_rows, ROWS_PER_DOT), jnp.float32),
+            pltpu.VMEM((n_samp - 1, part_rows, ROWS_PER_DOT), jnp.float32),
+            dma, dma((2,)),
+            dma((n_samp,)), dma((n_samp,)),
+            dma((n_samp,)), dma((n_samp,)),
+            dma((n_samp,)), dma((n_samp,)),
+        ],
+        compiler_params=pltpu.CompilerParams(
+            collective_id=0, has_side_effects=True, vmem_limit_bytes=VMEM_BYTES
+        ),
+        name="similarity",
+    )(vectors, partner, next_rows)
+    numerators = total[:groups].reshape(rows, cols)
+    own_totals = total[groups, :rows][:, None]
+    pair_totals = total[groups + 1, :cols][None, :]
+    return (2.0 * numerators / (own_totals + pair_totals), next_block)
+
+
+def body(n_vblk, n_samp, vectors, partner, next_rows):
+    rows, samples = vectors.shape
+    cols = rows // n_samp
+    fits = (
+        n_vblk > 2
+        and n_samp > 1
+        and n_samp & (n_samp - 1) == 0
+        and rows == ROWS_PER_DOT
+        and cols % SUB == 0
+        and samples % (TREE * KTILE) == 0
+        and next_rows.shape[0] % SUB == 0
+        and rows * SUB * samples * 2 + 4 * rows * samples * 2 <= VMEM_BYTES
+    )
+    if fits:
+        return fused_body(n_vblk, n_samp, vectors, partner, next_rows)
+    return plain_body(vectors, partner, next_rows)
+
+
 def solution(mesh):
     in_specs = (P("vblk", "samp"), P("vblk", "samp"), P(("vblk", "samp"), None))
     out_specs = (P("vblk", "samp"), P("vblk", "samp"))
-    return jax.shard_map(body, mesh=mesh, in_specs=in_specs, out_specs=out_specs, check_vma=False)
+    step = functools.partial(body, mesh.shape["vblk"], mesh.shape["samp"])
+    return jax.shard_map(step, mesh=mesh, in_specs=in_specs, out_specs=out_specs, check_vma=False)

time: 217 us -> 153 us (0.71)
  Pallas kernels: 0 us -> 146 us
  other arithmetic: 87.2 us -> 0.87 us
  waiting for transfers between devices: 51.5 us -> 0 us
  local copies, waits for them, and re-layouts: 37.6 us -> 5.28 us
  blocking collectives: 16 us -> 0 us
  between operations: 14.1 us -> 0.65 us
  starting transfers between devices: 7.97 us -> 0 us
    pallas_call x0 -> x1, Pallas kernels: none -> 146 us  [fused_body(): pl.pallas_call(functools.partial(kernel, n_vblk, n_samp), out_shape=(jax....]
    reduce_sum x34 -> x0, other arithmetic: 87.1 us -> none  [the longest x32 84.8 us: group_sums(): jnp.sum(jnp.minimum(row_group[:, None, :], col_block[None, :, :]), axis=2...]
    ppermute x1 -> x0, waiting for transfers between devices: 38.7 us -> none  [from_behind(): return lax.ppermute(value, axis, pairs)]
    min x32 -> x0, local copies, waits for them, and re-layouts: 27.1 us -> none  [group_sums(): jnp.minimum(row_group[:, None, :], col_block[None, :, :])]
    psum x1 -> x0, blocking collectives: 16 us -> none  [body(): row_totals = lax.psum(row_totals, 'samp')]
    unnamed x4 -> x0, waiting for transfers between devices: 12.8 us -> none
    all_to_all x1 -> x0, starting transfers between devices: 4.88 us -> none  [body(): lax.all_to_all(next_rows, 'samp', split_axis=1, concat_axis=0, tiled=True)]
    unnamed x6 -> x2, local copies, waits for them, and re-layouts: 7.12 us -> 3.82 us
  transfers between devices with their start and end apart: 4 -> 0, of which waited for: 2 -> 0; matrix products, arithmetic and copies ran while one was open for 57% -> 0% of each run, Pallas kernels for 0% -> 0%
where the time goes in v1:
time: 153 us
  Pallas kernels  146 us (95%)
  local copies, waits for them, and re-layouts  5.28 us (3%)
    pallas_call x1, Pallas kernels, fused_body(): pl.pallas_call(functools.partial(kernel, n_vblk, n_samp), out_shape=(jax....  146 us
    unnamed x2, local copies, waits for them, and re-layouts  3.82 us

profile of v1, /device:TPU:0, one launch (start us, length us, event | category | flops | bytes accessed | tf_op | source)
XLA Modules:
  0.0 153.0 jit_solution(14073486043520289014)
XLA Ops:
  0.6 146.2 %similarity.1 = (f32[40,256]{1,0:T(8,128)}, bf16[256,4096]{1,0:T(8,128)(2,1)}) custom-call(bf16[256,4096]{1,0:T(8,128)(2,1)} %vec_hbm.1, bf16[256,4096]{1,0:T(8,128)(2,1)} %partner_hbm.1, bf16[32,32768]{1,0:T(8,128)(2,1)} %next_hbm.1), custom_call_target="tpu_custom_call" | custom-call | tf_op jit(solution)/shard_map/similarity/pallas_call | solution.py:236
  146.9 0.8 slice_multiply_fusion
  147.6 0.1 mul.11
  147.7 0.7 slice.10
  148.4 0.7 slice_bitcast_fusion
  149.1 0.1 add_divide_fusion
  149.2 0.7 copy.6
  149.9 3.1 %copy.8 = bf16[256,4096]{1,0:T(8,128)(2,1)} copy(bf16[256,4096]{1,0:T(8,128)(2,1)} %get-tuple-element.11) | data formatting | bytes 4194304

commit v2 on v1

--- a/solution.py
+++ b/solution.py
@@ -8,8 +8,10 @@
 from jax.sharding import PartitionSpec as P
 
 MESH = pl.DeviceIdType.MESH
-SUB = 16
-LANES = 128
+SUB = 8
+ALIGN = 16
+WIDTH = 256
+UNROLL = 2
 TREE = 8
 KTILE = 256
 ROWS_PER_DOT = 256
@@ -148,17 +150,17 @@
     vec_copy.wait()
 
     def widen(t, carry):
-        first = pl.multiple_of(t * SUB, SUB)
-        for c in range(samples // LANES):
-            lanes = pl.ds(c * LANES, LANES)
-            rows = vec[pl.ds(first, SUB), lanes].astype(jnp.float32)
-            for r in range(SUB):
+        first = pl.multiple_of(t * ALIGN, ALIGN)
+        for c in range(samples // WIDTH):
+            lanes = pl.ds(c * WIDTH, WIDTH)
+            rows = vec[pl.ds(first, ALIGN), lanes].astype(jnp.float32)
+            for r in range(ALIGN):
                 wide[first + r, :, lanes] = jnp.broadcast_to(
-                    rows[r:r + 1, :], (SUB, LANES)
+                    rows[r:r + 1, :], (SUB, WIDTH)
                 ).astype(jnp.bfloat16)
         return carry
 
-    lax.fori_loop(0, row_count // SUB, widen, 0)
+    lax.fori_loop(0, row_count // ALIGN, widen, 0)
 
     own_totals = row_sums(vec[:, pl.ds(0, KTILE)])
     own_totals = lax.fori_loop(
@@ -175,30 +177,27 @@
         def one_group(q):
             out = None
             for kt in range(span // KTILE):
-                halves = []
-                for h in range(KTILE // LANES):
-                    at = [g * span + kt * KTILE + h * LANES for g in range(TREE)]
-                    theirs = [
-                        [arrived[i, pl.ds(j * SUB, SUB), pl.ds(o, LANES)] for o in at]
-                        for j in range(cols // SUB)
-                    ]
-                    pieces = []
+                at = [pl.ds(g * span + kt * KTILE, KTILE) for g in range(TREE)]
+                pieces = {}
+                for half in range(2):
+                    js = range(half * cols // SUB // 2, (half + 1) * cols // SUB // 2)
+                    theirs = {j: [arrived[i, pl.ds(j * SUB, SUB), o] for o in at] for j in js}
                     for r in range(group):
-                        mine = [wide[q * group + r, :, pl.ds(o, LANES)] for o in at]
-                        for j in range(cols // SUB):
-                            pieces.append(
-                                tree_sum([jnp.minimum(x, y) for x, y in zip(mine, theirs[j])])
+                        mine = [wide[q * group + r, :, o] for o in at]
+                        for j in js:
+                            pieces[r, j] = tree_sum(
+                                [jnp.minimum(x, y) for x, y in zip(mine, theirs[j])]
                             )
-                    halves.append(jnp.concatenate(pieces, axis=0))
-                sums = row_sums(jnp.concatenate(halves, axis=1))
+                sums = row_sums(jnp.concatenate([pieces[at_] for at_ in sorted(pieces)], axis=0))
                 out = sums if out is None else out + sums
             part[i, pl.ds(q, 1), :] = out[0:1, :]
 
         def groups_step(q, c):
-            one_group(q)
+            for k in range(UNROLL):
+                one_group(q * UNROLL + k)
             return c
 
-        lax.fori_loop(0, groups, groups_step, 0)
+        lax.fori_loop(0, groups // UNROLL, groups_step, 0)
         part[i, pl.ds(groups, 8), :] = own_totals
         part[i, pl.ds(groups + 1, 1), pl.ds(0, cols)] = row_sums(arrived[i])[0:1, :]
 
@@ -272,9 +271,9 @@
         and n_samp > 1
         and n_samp & (n_samp - 1) == 0
         and rows == ROWS_PER_DOT
-        and cols % SUB == 0
+        and cols % ALIGN == 0
         and samples % (TREE * KTILE) == 0
-        and next_rows.shape[0] % SUB == 0
+        and next_rows.shape[0] % ALIGN == 0
         and rows * SUB * samples * 2 + 4 * rows * samples * 2 <= VMEM_BYTES
     )
     if fits:

time: 153 us -> 80.2 us (0.52)
  Pallas kernels: 146 us -> 73.1 us
    pallas_call x1, Pallas kernels: 146 us -> 73.1 us  [fused_body(): pl.pallas_call(functools.partial(kernel, n_vblk, n_samp), out_shape=(jax....]
where the time goes in v2:
time: 80.2 us; the launch traced here: 79.9 us
  Pallas kernels  73.1 us (91%)
  local copies, waits for them, and re-layouts  5.28 us (7%)
  other arithmetic  0.87 us (1%)
    pallas_call x1, Pallas kernels, fused_body(): pl.pallas_call(functools.partial(kernel, n_vblk, n_samp), out_shape=(jax....  73.1 us
    unnamed x2, local copies, waits for them, and re-layouts  3.82 us

profile of v2, /device:TPU:0, one launch (start us, length us, event | category | flops | bytes accessed | tf_op | source)
XLA Modules:
  0.0 79.9 jit_solution(13718075472922338491)
XLA Ops:
  0.6 73.1 %similarity.1 = (f32[40,256]{1,0:T(8,128)}, bf16[256,4096]{1,0:T(8,128)(2,1)}) custom-call(bf16[256,4096]{1,0:T(8,128)(2,1)} %vec_hbm.1, bf16[256,4096]{1,0:T(8,128)(2,1)} %partner_hbm.1, bf16[32,32768]{1,0:T(8,128)(2,1)} %next_hbm.1), custom_call_target="tpu_custom_call" | custom-call | tf_op jit(solution)/shard_map/similarity/pallas_call | solution.py:235
  73.8 0.8 slice_multiply_fusion
  74.5 0.1 mul.11
  74.6 0.7 slice.10
  75.3 0.7 slice_bitcast_fusion
  76.0 0.1 add_divide_fusion
  76.1 0.7 copy.6
  76.8 3.1 %copy.8 = bf16[256,4096]{1,0:T(8,128)(2,1)} copy(bf16[256,4096]{1,0:T(8,128)(2,1)} %get-tuple-element.11) | data formatting | bytes 4194304

commit v3 on v2

--- a/solution.py
+++ b/solution.py
@@ -177,18 +177,19 @@
         def one_group(q):
             out = None
             for kt in range(span // KTILE):
-                at = [pl.ds(g * span + kt * KTILE, KTILE) for g in range(TREE)]
+                at = [pl.ds((kt * TREE + g) * KTILE, KTILE) for g in range(TREE)]
                 pieces = {}
                 for half in range(2):
                     js = range(half * cols // SUB // 2, (half + 1) * cols // SUB // 2)
                     theirs = {j: [arrived[i, pl.ds(j * SUB, SUB), o] for o in at] for j in js}
                     for r in range(group):
-                        mine = [wide[q * group + r, :, o] for o in at]
+                        mine = [wide[r * groups + q, :, o] for o in at]
                         for j in js:
                             pieces[r, j] = tree_sum(
                                 [jnp.minimum(x, y) for x, y in zip(mine, theirs[j])]
                             )
-                sums = row_sums(jnp.concatenate([pieces[at_] for at_ in sorted(pieces)], axis=0))
+                minima = jnp.stack([pieces[key] for key in sorted(pieces)])
+                sums = row_sums(minima.reshape(ROWS_PER_DOT, KTILE))
                 out = sums if out is None else out + sums
             part[i, pl.ds(q, 1), :] = out[0:1, :]
 
@@ -222,6 +223,35 @@
     for m in range(1, n_samp):
         next_copy(m).wait()
     own_out.wait()
+
+
+def finish(groups, cols, total_ref, block_in, metric_ref, block_out, pieces, in_sems, out_sems):
+    count, rows, _ = pieces.shape
+
+    def take(i):
+        return pltpu.make_async_copy(
+            block_in.at[pl.ds(i * rows, rows), :], pieces.at[i], in_sems.at[i]
+        )
+
+    def give(i):
+        return pltpu.make_async_copy(
+            pieces.at[i], block_out.at[pl.ds(i * rows, rows), :], out_sems.at[i]
+        )
+
+    for i in range(count):
+        take(i).start()
+    turned = total_ref[pl.ds(0, groups), :].T
+    numerators = jnp.concatenate(
+        [turned[first:first + cols, :] for first in range(0, turned.shape[0], cols)], axis=1
+    )
+    own_totals = total_ref[pl.ds(groups, 1), :]
+    pair_totals = total_ref[pl.ds(groups, 8), :].T[:cols, 1:2]
+    metric_ref[...] = 2.0 * numerators / (own_totals + pair_totals)
+    for i in range(count):
+        take(i).wait()
+        give(i).start()
+    for i in range(count):
+        give(i).wait()
 
 
 def fused_body(n_vblk, n_samp, vectors, partner, next_rows):
@@ -257,10 +287,21 @@
         ),
         name="similarity",
     )(vectors, partner, next_rows)
-    numerators = total[:groups].reshape(rows, cols)
-    own_totals = total[groups, :rows][:, None]
-    pair_totals = total[groups + 1, :cols][None, :]
-    return (2.0 * numerators / (own_totals + pair_totals), next_block)
+    metric, next_block = pl.pallas_call(
+        functools.partial(finish, groups, cols),
+        out_shape=(
+            jax.ShapeDtypeStruct((cols, rows), jnp.float32),
+            jax.ShapeDtypeStruct(next_block.shape, next_block.dtype),
+        ),
+        in_specs=[pl.BlockSpec(memory_space=pltpu.VMEM), hbm],
+        out_specs=(pl.BlockSpec(memory_space=pltpu.VMEM), hbm),
+        scratch_shapes=[
+            pltpu.VMEM((n_samp, next_count, samples), next_rows.dtype),
+            dma((n_samp,)), dma((n_samp,)),
+        ],
+        name="finish",
+    )(total, next_block)
+    return (metric.T, next_block)
 
 
 def body(n_vblk, n_samp, vectors, partner, next_rows):
@@ -275,6 +316,7 @@
         and samples % (TREE * KTILE) == 0
         and next_rows.shape[0] % ALIGN == 0
         and rows * SUB * samples * 2 + 4 * rows * samples * 2 <= VMEM_BYTES
+        and next_rows.shape[0] * n_samp == rows
     )
     if fits:
         return fused_body(n_vblk, n_samp, vectors, partner, next_rows)

time: 80.2 us -> 73.3 us (0.914)
  local copies, waits for them, and re-layouts: 5.28 us -> 0 us
  other arithmetic: 0.87 us -> 0 us
    pallas_call x1, Pallas kernels: 73.1 us -> 68.7 us  [fused_body(): pl.pallas_call(functools.partial(kernel, n_vblk, n_samp), out_shape=(jax....]
    unnamed x2 -> x0, local copies, waits for them, and re-layouts: 3.82 us -> none
    pallas_call x0 -> x1, Pallas kernels: none -> 3.79 us  [fused_body(): pl.pallas_call(functools.partial(finish, groups, cols), out_shape=(jax.Sh...]
where the time goes in v3:
time: 73.3 us; the launch traced here: 73.1 us
  Pallas kernels  72.5 us (99%)
    pallas_call x1, Pallas kernels, fused_body(): pl.pallas_call(functools.partial(kernel, n_vblk, n_samp), out_shape=(jax....  68.7 us
    pallas_call x1, Pallas kernels, fused_body(): pl.pallas_call(functools.partial(finish, groups, cols), out_shape=(jax.Sh...  3.79 us

profile of v3, /device:TPU:0, one launch (start us, length us, event | category | flops | bytes accessed | tf_op | source)
XLA Modules:
  0.0 73.1 jit_solution(15384449089800806189)
XLA Ops:
  0.6 68.7 %similarity.1 = (f32[40,256]{1,0:T(8,128)}, bf16[256,4096]{1,0:T(8,128)(2,1)}) custom-call(bf16[256,4096]{1,0:T(8,128)(2,1)} %vec_hbm.1, bf16[256,4096]{1,0:T(8,128)(2,1)} %partner_hbm.1, bf16[32,32768]{1,0:T(8,128)(2,1)} %next_hbm.1), custom_call_target="tpu_custom_call" | custom-call | tf_op jit(solution)/shard_map/similarity/pallas_call | solution.py:265
  69.3 3.8 %finish.1 = (f32[32,256]{1,0:T(8,128)}, bf16[256,4096]{1,0:T(8,128)(2,1)}) custom-call(f32[40,256]{1,0:T(8,128)} %get-tuple-element.6.total_ref, bf16[256,4096]{1,0:T(8,128)(2,1)} %get-tuple-element.7.block_in), custom_call_target="tpu_custom_call" | custom-call | tf_op jit(solution)/shard_map/finish/pallas_call | solution.py:290

commit v4 on v3

--- a/solution.py
+++ b/solution.py
@@ -11,7 +11,7 @@
 SUB = 8
 ALIGN = 16
 WIDTH = 256
-UNROLL = 2
+UNROLL = 8
 TREE = 8
 KTILE = 256
 ROWS_PER_DOT = 256
@@ -225,7 +225,10 @@
     own_out.wait()
 
 
-def finish(groups, cols, total_ref, block_in, metric_ref, block_out, pieces, in_sems, out_sems):
+def finish(
+    groups, cols, total_hbm, block_in, metric_hbm, block_out,
+    total_ref, metric_ref, pieces, in_sems, out_sems, end_sems,
+):
     count, rows, _ = pieces.shape
 
     def take(i):
@@ -238,8 +241,12 @@
             pieces.at[i], block_out.at[pl.ds(i * rows, rows), :], out_sems.at[i]
         )
 
+    total_in = pltpu.make_async_copy(total_hbm, total_ref, end_sems.at[0])
+    metric_out = pltpu.make_async_copy(metric_ref, metric_hbm, end_sems.at[1])
+    total_in.start()
     for i in range(count):
         take(i).start()
+    total_in.wait()
     turned = total_ref[pl.ds(0, groups), :].T
     numerators = jnp.concatenate(
         [turned[first:first + cols, :] for first in range(0, turned.shape[0], cols)], axis=1
@@ -247,11 +254,13 @@
     own_totals = total_ref[pl.ds(groups, 1), :]
     pair_totals = total_ref[pl.ds(groups, 8), :].T[:cols, 1:2]
     metric_ref[...] = 2.0 * numerators / (own_totals + pair_totals)
+    metric_out.start()
     for i in range(count):
         take(i).wait()
         give(i).start()
     for i in range(count):
         give(i).wait()
+    metric_out.wait()
 
 
 def fused_body(n_vblk, n_samp, vectors, partner, next_rows):
@@ -293,11 +302,13 @@
             jax.ShapeDtypeStruct((cols, rows), jnp.float32),
             jax.ShapeDtypeStruct(next_block.shape, next_block.dtype),
         ),
-        in_specs=[pl.BlockSpec(memory_space=pltpu.VMEM), hbm],
-        out_specs=(pl.BlockSpec(memory_space=pltpu.VMEM), hbm),
+        in_specs=[hbm, hbm],
+        out_specs=(hbm, hbm),
         scratch_shapes=[
+            pltpu.VMEM((part_rows, ROWS_PER_DOT), jnp.float32),
+            pltpu.VMEM((cols, rows), jnp.float32),
             pltpu.VMEM((n_samp, next_count, samples), next_rows.dtype),
-            dma((n_samp,)), dma((n_samp,)),
+            dma((n_samp,)), dma((n_samp,)), dma((2,)),
         ],
         name="finish",
     )(total, next_block)
@@ -313,6 +324,7 @@
         and n_samp & (n_samp - 1) == 0
         and rows == ROWS_PER_DOT
         and cols % ALIGN == 0
+        and cols % UNROLL == 0
         and samples % (TREE * KTILE) == 0
         and next_rows.shape[0] % ALIGN == 0
         and rows * SUB * samples * 2 + 4 * rows * samples * 2 <= VMEM_BYTES

time: 73.3 us -> 64.1 us (0.87)
  Pallas kernels: 72.5 us -> 63.4 us
    pallas_call x1, Pallas kernels: 68.7 us -> 60.3 us  [fused_body(): pl.pallas_call(functools.partial(kernel, n_vblk, n_samp), out_shape=(jax....]
    pallas_call x1, Pallas kernels: 3.79 us -> 3.04 us  [fused_body(): pl.pallas_call(functools.partial(finish, groups, cols), out_shape=(jax.Sh...]
where the time goes in v4:
time: 64.1 us; the launch traced here: 64 us
  Pallas kernels  63.4 us (99%)
    pallas_call x1, Pallas kernels, fused_body(): pl.pallas_call(functools.partial(kernel, n_vblk, n_samp), out_shape=(jax....  60.3 us
    pallas_call x1, Pallas kernels, fused_body(): pl.pallas_call(functools.partial(finish, groups, cols), out_shape=(jax.Sh...  3.04 us

profile of v4, /device:TPU:0, one launch (start us, length us, event | category | flops | bytes accessed | tf_op | source)
XLA Modules:
  0.0 64.0 jit_solution(16780115533162959348)
XLA Ops:
  0.6 60.3 %similarity.1 = (f32[40,256]{1,0:T(8,128)}, bf16[256,4096]{1,0:T(8,128)(2,1)}) custom-call(bf16[256,4096]{1,0:T(8,128)(2,1)} %vec_hbm.1, bf16[256,4096]{1,0:T(8,128)(2,1)} %partner_hbm.1, bf16[32,32768]{1,0:T(8,128)(2,1)} %next_hbm.1), custom_call_target="tpu_custom_call" | custom-call | tf_op jit(solution)/shard_map/similarity/pallas_call | solution.py:274
  61.0 3.0 %finish.1 = (f32[32,256]{1,0:T(8,128)}, bf16[256,4096]{1,0:T(8,128)(2,1)}) custom-call(f32[40,256]{1,0:T(8,128)} %get-tuple-element.6.total_hbm, bf16[256,4096]{1,0:T(8,128)(2,1)} %get-tuple-element.7.block_in), custom_call_target="tpu_custom_call" | custom-call | tf_op jit(solution)/shard_map/finish/pallas_call | solution.py:299
